TPU v7x, 32 devices: a whole 2x2x4 slice. The times are simulated.
32 devices in a mesh: grp: 2 (over core), ex: 16 (over z, y, x).
Axes of the slice: x: 2, y: 2, z: 4, core: 2. Of those that a mesh axis runs over, the one named last changes fastest.
Arguments:
- tokens: bfloat16 [8192, 1024], P(('grp', 'ex')), may hold values from -6 to 6
- expert_ids: int32 [8192], P(('grp', 'ex')), may hold values from 0 to 15, as said below
- slot_ids: int32 [8192], P(('grp', 'ex')), may hold values from 0 to 31, as said below
- centroids: bfloat16 [16, 1024], replicated, may hold values from -0.1875 to 0.1875
- w_in: bfloat16 [16, 1024, 4096], P('ex', None, 'grp'), may hold values from -0.1875 to 0.1875
- w_out: bfloat16 [16, 4096, 1024], P('ex', 'grp'), may hold values from -0.09375 to 0.09375
Outputs:
- combined: bfloat16 [8192, 1024], P(('grp', 'ex'))
Inputs may be any that keep to these rules, and one draw needn't show every extreme that they name: `expert_ids`: within each device's 256 rows, at most 32 rows name one expert; in every device some expert is named by exactly 32 rows, and in each group of 16 devices along ex one expert is named by 32 rows on every device of the group. `slot_ids`: rows of one device that name the same expert have distinct slots.
All inputs are finite; a program needn't handle non-finite values.
Results may differ from a plain program's by a relative error of at most 0.0035.
Values may be sent and summed in bfloat16 or wider, within the bound.
A program may use at most 128 MiB of HBM per device.

v0:
```python
import functools

import jax
import jax.numpy as jnp
from jax import lax
from jax.experimental import pallas as pl
from jax.experimental.pallas import tpu as pltpu
from jax.sharding import PartitionSpec as P

MESH = pl.DeviceIdType.MESH
TILE = 1024


def expert_kernel(
    n,
    cap,
    ids_ref,
    slots_ref,
    tokens_hbm,
    centroids_ref,
    w_in_ref,
    w_out_ref,
    out_ref,
    outgoing,
    received,
    result,
    returned,
    total,
    tokens_ref,
    place,
    columns,
    full_in,
    full_out,
    load_sem,
    share_send,
    share_recv,
    send_sem,
    recv_sem,
    back_send,
    back_recv,
):
    grp = lax.axis_index("grp")
    me = lax.axis_index("ex")
    half = n // 2
    side = me // half
    seat = me % half
    quarter = n // 4
    rows = quarter * cap
    tokens_here, width = tokens_ref.shape
    hidden = full_in.shape[2]

    def peer_to(slot):
        return ((side + slot // half) % 2) * half + (seat + slot % half) % half

    def peer_from(slot):
        return ((side + slot // half) % 2) * half + (seat + half - slot % half) % half

    def block(slot):
        start = slot * cap
        if not isinstance(slot, int):
            start = pl.multiple_of(start, cap)
        return pl.ds(start, cap)

    barrier = pltpu.get_barrier_semaphore()
    for slot in range(1, n):
        pl.semaphore_signal(
            barrier, inc=1, device_id={"ex": peer_to(slot)}, device_id_type=MESH
        )
    pl.semaphore_signal(barrier, inc=1, device_id={"grp": 1 - grp}, device_id_type=MESH)

    bring = pltpu.make_async_copy(tokens_hbm, tokens_ref, load_sem.at[2])
    bring.start()
    loads = [
        pltpu.make_async_copy(w_in_ref.at[0], full_in.at[0], load_sem.at[0]),
        pltpu.make_async_copy(w_out_ref.at[0], full_out.at[0], load_sem.at[1]),
    ]
    for load in loads:
        load.start()

    ids = ids_ref[...]
    high = (ids >= half).astype(jnp.int32)
    ahead = ids - high * half - seat
    ahead = jnp.where(ahead < 0, ahead + half, ahead)
    across = jnp.where(high == side, 0, 1)
    position = (across * half + ahead) * cap + slots_ref[...]
    slot_rows = lax.broadcasted_iota(jnp.int32, (n * cap, tokens_here), 0)
    spread = (slot_rows == position).astype(jnp.bfloat16)
    bring.wait()
    packed = jnp.dot(spread, tokens_ref[...], preferred_element_type=jnp.float32)
    packed = packed.astype(jnp.bfloat16)
    outgoing[...] = packed
    received[block(0), :] = packed[:cap]

    shares = [
        pltpu.make_async_remote_copy(
            src_ref=w_in_ref.at[0],
            dst_ref=full_in.at[1],
            send_sem=share_send.at[0],
            recv_sem=share_recv.at[0],
            device_id={"grp": 1 - grp},
            device_id_type=MESH,
        ),
        pltpu.make_async_remote_copy(
            src_ref=w_out_ref.at[0],
            dst_ref=full_out.at[1],
            send_sem=share_send.at[1],
            recv_sem=share_recv.at[1],
            device_id={"grp": 1 - grp},
            device_id_type=MESH,
        ),
    ]

    def dispatch(slot):
        return pltpu.make_async_remote_copy(
            src_ref=outgoing.at[block(slot), :],
            dst_ref=received.at[block(slot), :],
            send_sem=send_sem.at[slot],
            recv_sem=recv_sem.at[slot],
            device_id={"ex": peer_to(slot)},
            device_id_type=MESH,
        )

    def give_back(slot):
        return pltpu.make_async_remote_copy(
            src_ref=result.at[block(slot), :],
            dst_ref=returned.at[block(slot), :],
            send_sem=back_send.at[slot],
            recv_sem=back_recv.at[slot],
            device_id={"ex": peer_from(slot)},
            device_id_type=MESH,
        )

    pl.semaphore_wait(barrier, n)
    for step in reversed(range(half)):
        dispatch(half + step).start()
        if step > 0:
            dispatch(step).start()
    for share in shares:
        share.start()

    scores = lax.dot_general(
        centroids_ref[...],
        tokens_ref[...],
        (((1,), (1,)), ((), ())),
        preferred_element_type=jnp.float32,
    )
    experts = lax.broadcasted_iota(jnp.int32, scores.shape, 0)
    chosen = jnp.sum(jnp.where(experts == ids, scores, 0.0), axis=0, keepdims=True)
    gating = 1.0 / (1.0 + jnp.exp(-chosen))
    lines = lax.broadcasted_iota(jnp.int32, (128, tokens_here), 0)
    columns[...] = jnp.where(lines == 0, position.astype(jnp.float32), gating).T
    slot_columns = lax.broadcasted_iota(jnp.int32, (tokens_here, n * cap), 1)
    place[...] = (slot_columns == columns[:, 0:1].astype(jnp.int32)).astype(jnp.bfloat16)

    for load in loads:
        load.wait()
    for share in shares:
        share.wait_recv()

    @pl.loop(0, 4)
    def _(turn):
        chunk = 3 - (2 * turn) % 4 - turn // 2
        first = chunk * quarter

        @pl.loop(0, quarter)
        def _(k):
            @pl.when(first + k > 0)
            def _():
                dispatch(first + k).wait_recv()

        here = pl.ds(pl.multiple_of(chunk * rows, rows), rows)
        total[...] = jnp.zeros_like(total)

        @pl.loop(0, 2 * (hidden // TILE))
        def _(piece):
            part = piece // (hidden // TILE)
            cut = pl.ds(pl.multiple_of((piece % (hidden // TILE)) * TILE, TILE), TILE)
            middle = jnp.dot(
                received[here, :], full_in[part, :, cut], preferred_element_type=jnp.float32
            )
            middle = jnp.maximum(middle, 0.0).astype(jnp.bfloat16)
            total[...] += jnp.dot(
                middle, full_out[part, cut, :], preferred_element_type=jnp.float32
            )

        result[here, :] = total[...].astype(jnp.bfloat16)

        @pl.loop(0, quarter)
        def _(k):
            @pl.when(first + k > 0)
            def _():
                give_back(first + k).start()

            @pl.when(first + k == 0)
            def _():
                returned[block(0), :] = result[block(0), :]

    arrived = jnp.zeros((tokens_here, width), jnp.float32)
    for chunk in (1, 3, 0, 2):
        for slot in range(chunk * quarter, (chunk + 1) * quarter):
            if slot > 0:
                give_back(slot).wait_recv()
        here = pl.ds(chunk * rows, rows)
        arrived += jnp.dot(
            place[:, here], returned[here, :], preferred_element_type=jnp.float32
        )
    mixed = tokens_ref[...].astype(jnp.float32) + columns[:, 1:2] * arrived
    out_ref[...] = mixed.astype(jnp.bfloat16)

    @pl.loop(1, n)
    def _(slot):
        dispatch(slot).wait_send()
        give_back(slot).wait_send()

    for share in shares:
        share.wait_send()


def in_one_kernel(n, tokens, expert_ids, slot_ids, centroids, w_in, w_out):
    count, width = tokens.shape
    cap = 2 * count // n
    slots = n * cap
    rows = slots // 4
    hidden = w_in.shape[2]
    vmem = pl.BlockSpec(memory_space=pltpu.VMEM)
    hbm = pl.BlockSpec(memory_space=pl.ANY)
    sems = pltpu.SemaphoreType.DMA
    return pl.pallas_call(
        functools.partial(expert_kernel, n, cap),
        out_shape=pltpu.VMEM((count, width), jnp.bfloat16),
        in_specs=[vmem, vmem, hbm, vmem, hbm, hbm],
        out_specs=vmem,
        scratch_shapes=[
            pltpu.VMEM((slots, width), jnp.bfloat16),
            pltpu.VMEM((slots, width), jnp.bfloat16),
            pltpu.VMEM((slots, width), jnp.bfloat16),
            pltpu.VMEM((slots, width), jnp.bfloat16),
            pltpu.VMEM((rows, width), jnp.float32),
            pltpu.VMEM((count, width), jnp.bfloat16),
            pltpu.VMEM((count, slots), jnp.bfloat16),
            pltpu.VMEM((count, 128), jnp.float32),
            pltpu.VMEM((2, width, hidden), jnp.bfloat16),
            pltpu.VMEM((2, hidden, width), jnp.bfloat16),
            sems((3,)),
            sems((2,)),
            sems((2,)),
            sems((n,)),
            sems((n,)),
            sems((n,)),
            sems((n,)),
        ],
        compiler_params=pltpu.CompilerParams(
            collective_id=0, has_side_effects=True, vmem_limit_bytes=60 * 1024 * 1024
        ),
    )(
        expert_ids.reshape(1, count),
        slot_ids.reshape(1, count),
        tokens,
        centroids,
        w_in,
        w_out,
    )


def in_plain_ops(tokens, expert_ids, slot_ids, centroids, w_in, w_out):
    experts = centroids.shape[0]
    count_rows = tokens.shape[0]
    model_width = tokens.shape[1]
    capacity = 2 * count_rows // experts
    buffer_rows = expert_ids * capacity + slot_ids
    outgoing = (
        jnp.zeros((experts * capacity, model_width), jnp.bfloat16).at[buffer_rows].set(tokens)
    )
    outgoing = outgoing.reshape(experts, capacity, model_width)
    scores = jnp.dot(tokens, centroids.T, preferred_element_type=jnp.float32)
    columns = jnp.arange(experts, dtype=jnp.int32)
    chosen = jnp.sum(jnp.where(columns[None, :] == expert_ids[:, None], scores, 0.0), axis=1)
    gating = jax.nn.sigmoid(chosen)
    full_in, full_out = (
        lax.all_gather(w_in, "grp", axis=2, tiled=True),
        lax.all_gather(w_out, "grp", axis=1, tiled=True),
    )
    received = lax.all_to_all(outgoing, "ex", split_axis=0, concat_axis=0, tiled=True)
    flat_rows = received.reshape(-1, model_width)
    hidden = jnp.maximum(
        jnp.dot(flat_rows, full_in[0], preferred_element_type=jnp.float32), 0.0
    ).astype(jnp.bfloat16)
    result = jnp.dot(hidden, full_out[0], preferred_element_type=jnp.float32)
    returned = lax.all_to_all(
        result.astype(jnp.bfloat16).reshape(received.shape),
        "ex",
        split_axis=0,
        concat_axis=0,
        tiled=True,
    )
    arrived = returned.reshape(-1, model_width)[buffer_rows]
    mixed_rows = tokens.astype(jnp.float32) + gating[:, None] * arrived.astype(jnp.float32)
    return mixed_rows.astype(jnp.bfloat16)


def solution(mesh):
    n = mesh.shape["ex"]

    def on_device(tokens, expert_ids, slot_ids, centroids, w_in, w_out):
        capacity = 2 * tokens.shape[0] // n
        if mesh.shape["grp"] == 2 and n % 4 == 0 and capacity % 16 == 0:
            return in_one_kernel(n, tokens, expert_ids, slot_ids, centroids, w_in, w_out)
        return in_plain_ops(tokens, expert_ids, slot_ids, centroids, w_in, w_out)

    in_specs = (
        P(("grp", "ex"), None),
        P(("grp", "ex")),
        P(("grp", "ex")),
        P(),
        P("ex", None, "grp"),
        P("ex", "grp", None),
    )
    out_specs = P(("grp", "ex"), None)
    return jax.shard_map(
        on_device, mesh=mesh, in_specs=in_specs, out_specs=out_specs, check_vma=False
    )
```

profile of v0, /device:TPU:0, one launch (start us, length us, event | category | flops | bytes accessed | tf_op | source)
XLA Modules:
  0.0 55.9 jit_solution(4677579809490418733)
XLA Ops:
  0.0 55.1 %shard_map.64 = bf16[256,1024]{1,0:T(8,128)(2,1)S(1)} custom-call(s32[1,256]{1,0:T(1,128)} %bitcast.2, s32[1,256]{1,0:T(1,128)} %bitcast.3, bf16[256,1024]{1,0:T(8,128)(2,1)} %tokens_hbm.1, bf16[16,1024]{1,0:T(8,128)(2,1)} %centroids_ref.1, bf16[1,1024,2048]{2,1,0:T(8,128)(2,1)} %w_in_ref.1, bf16[1,2048,1024]{2,1,0:T(8,128)(2,1)} %w_out_ref.1), custom_call_target="tpu_custom_call" | custom-call | tf_op jit(solution)/shard_map/pallas_call | solution.py:228
  55.1 0.8 %copy.8 = bf16[256,1024]{1,0:T(8,128)(2,1)} copy(bf16[256,1024]{1,0:T(8,128)(2,1)S(1)} %shard_map.64) | data formatting | bytes 1048576
where the time goes:
time: 56.1 us; the launch traced here: 55.9 us
  Pallas kernels  55.1 us (98%)
  local copies, waits for them, and re-layouts  0.8 us (1%)
    pallas_call x1, Pallas kernels, in_one_kernel(): pl.pallas_call(functools.partial(expert_kernel, n, cap), out_shape=pltpu....  55.1 us

commit v1 on v0

--- a/solution.py
+++ b/solution.py
@@ -9,6 +9,8 @@
 
 MESH = pl.DeviceIdType.MESH
 TILE = 1024
+ORDER = (1, 3, 2, "home", 0)
+FINISH = (1, 2, 0, 3)
 
 
 def expert_kernel(
@@ -262,6 +264,439 @@
     )
 
 
+def relay_kernel(
+    n,
+    cap,
+    spare,
+    ids_ref,
+    slots_ref,
+    tokens_hbm,
+    centroids_ref,
+    w_in_ref,
+    w_out_ref,
+    out_ref,
+    spill_ref,
+    outgoing,
+    pouch,
+    inbox,
+    expanded,
+    received,
+    result,
+    collected,
+    returned,
+    total,
+    tokens_ref,
+    place,
+    columns,
+    full_in,
+    full_out,
+    flag_out,
+    flags_in,
+    group_out,
+    group_in,
+    load_sem,
+    share_send,
+    share_recv,
+    send_sem,
+    recv_sem,
+    back_send,
+    back_recv,
+    relay_send,
+    relay_recv,
+    relay_back_send,
+    relay_back_recv,
+    pouch_send,
+    pouch_recv,
+    flag_send,
+    flag_recv,
+):
+    grp = lax.axis_index("grp")
+    me = lax.axis_index("ex")
+    half = n // 2
+    base = cap // 2
+    side = me // half
+    seat = me % half
+    mirror = (1 - side) * half + seat
+    near_rows = half * cap
+    far_rows = half * base
+    direct_rows = near_rows + far_rows
+    rows = near_rows // 2
+    tokens_here, width = tokens_ref.shape
+    hidden = full_in.shape[2]
+    pieces = hidden // TILE
+
+    def peer_to(slot):
+        return ((side + slot // half) % 2) * half + (seat + slot % half) % half
+
+    def peer_from(slot):
+        return ((side + slot // half) % 2) * half + (seat + half - slot % half) % half
+
+    def block(slot):
+        if slot < half:
+            return pl.ds(slot * cap, cap)
+        return pl.ds(near_rows + (slot - half) * base, base)
+
+    def extra(k, start=0):
+        return pl.ds(start + k * base, base)
+
+    def remote(src, dst, send, recv, where):
+        return pltpu.make_async_remote_copy(
+            src_ref=src,
+            dst_ref=dst,
+            send_sem=send,
+            recv_sem=recv,
+            device_id=where,
+            device_id_type=MESH,
+        )
+
+    def dispatch(slot):
+        return remote(
+            outgoing.at[block(slot), :],
+            received.at[block(slot), :],
+            send_sem.at[slot],
+            recv_sem.at[slot],
+            {"ex": peer_to(slot)},
+        )
+
+    def give_back(slot):
+        return remote(
+            result.at[block(slot), :],
+            returned.at[block(slot), :],
+            back_send.at[slot],
+            back_recv.at[slot],
+            {"ex": peer_from(slot)},
+        )
+
+    def forward(k):
+        return remote(
+            expanded.at[extra(k), :],
+            received.at[extra(k, direct_rows), :],
+            relay_send.at[k],
+            relay_recv.at[k],
+            {"ex": peer_to(k)},
+        )
+
+    def give_relay(k):
+        return remote(
+            result.at[extra(k, direct_rows), :],
+            collected.at[extra(k), :],
+            relay_back_send.at[k],
+            relay_back_recv.at[k],
+            {"ex": peer_from(k)},
+        )
+
+    send_pouch = remote(pouch, inbox, pouch_send.at[0], pouch_recv.at[0], {"ex": mirror})
+    back_pouch = remote(
+        expanded.at[pl.ds(0, spare), :],
+        returned.at[pl.ds(direct_rows, spare), :],
+        pouch_send.at[1],
+        pouch_recv.at[1],
+        {"ex": mirror},
+    )
+
+    def send_flag(slot):
+        return remote(
+            flag_out, flags_in.at[slot], flag_send.at[slot], flag_recv.at[slot], {"ex": peer_to(slot)}
+        )
+
+    swap_flag = remote(group_out, group_in, flag_send.at[0], flag_recv.at[0], {"grp": 1 - grp})
+
+    barrier = pltpu.get_barrier_semaphore()
+    for slot in range(1, n):
+        pl.semaphore_signal(
+            barrier, inc=1, device_id={"ex": peer_to(slot)}, device_id_type=MESH
+        )
+    pl.semaphore_signal(barrier, inc=1, device_id={"grp": 1 - grp}, device_id_type=MESH)
+
+    bring = pltpu.make_async_copy(tokens_hbm, tokens_ref, load_sem.at[2])
+    bring.start()
+    loads = [
+        pltpu.make_async_copy(w_in_ref.at[0], full_in.at[0], load_sem.at[0]),
+        pltpu.make_async_copy(w_out_ref.at[0], full_out.at[0], load_sem.at[1]),
+    ]
+    for load in loads:
+        load.start()
+
+    ids = ids_ref[...]
+    slots = slots_ref[...]
+    high = (ids >= half).astype(jnp.int32)
+    ahead = ids - high * half - seat
+    ahead = jnp.where(ahead < 0, ahead + half, ahead)
+    across = high != side
+    order = (ids * cap + slots).astype(jnp.float32)
+    floor = (ids * cap).astype(jnp.float32)
+    columns[...] = jnp.broadcast_to(order, (128, tokens_here)).T
+    order_column = columns[:, 0:1]
+    before = jnp.logical_and(order_column >= floor, order_column < order)
+    rank = jnp.sum(jnp.where(before, 1.0, 0.0), axis=0, keepdims=True)
+    rank = rank.astype(jnp.int32)
+    late = jnp.logical_and(across, rank >= base)
+    lines = lax.broadcasted_iota(jnp.int32, (tokens_here, tokens_here), 0)
+    lanes = lax.broadcasted_iota(jnp.int32, (tokens_here, tokens_here), 1)
+    earlier = (lines < lanes).astype(jnp.bfloat16)
+    marks = jnp.broadcast_to(jnp.where(late, 1.0, 0.0), (16, tokens_here)).astype(jnp.bfloat16)
+    queue = jnp.dot(marks, earlier, preferred_element_type=jnp.float32)[0:1, :]
+    queue = queue.astype(jnp.int32)
+    position = jnp.where(
+        across,
+        jnp.where(late, direct_rows + queue, near_rows + ahead * base + rank),
+        ahead * cap + slots,
+    )
+    spill = jnp.max(jnp.where(late, queue + 1, 0), axis=1, keepdims=True) > spare
+    flag_out[...] = jnp.broadcast_to(jnp.where(spill, 1.0, 0.0), flag_out.shape)
+    flags_in[0] = flag_out[...]
+
+    slot_rows = lax.broadcasted_iota(jnp.int32, (direct_rows + spare, tokens_here), 0)
+    hits = slot_rows == position
+    spread = hits.astype(jnp.bfloat16)
+    target = (ahead * base + rank - base + 1).astype(jnp.float32)
+    aim = jnp.sum(jnp.where(hits[direct_rows:], target, 0.0), axis=1, keepdims=True)
+    wide = lax.broadcasted_iota(jnp.int32, (spare, 128), 1).astype(jnp.float32)
+    pouch[:, width:] = (wide == aim - 1.0).astype(jnp.bfloat16)
+    bring.wait()
+    packed = jnp.dot(spread, tokens_ref[...], preferred_element_type=jnp.float32)
+    packed = packed.astype(jnp.bfloat16)
+    outgoing[...] = packed[:direct_rows]
+    pouch[:, :width] = packed[direct_rows:]
+    received[block(0), :] = packed[:cap]
+
+    shares = [
+        remote(
+            w_in_ref.at[0],
+            full_in.at[1],
+            share_send.at[0],
+            share_recv.at[0],
+            {"grp": 1 - grp},
+        ),
+        remote(
+            w_out_ref.at[0],
+            full_out.at[1],
+            share_send.at[1],
+            share_recv.at[1],
+            {"grp": 1 - grp},
+        ),
+    ]
+
+    pl.semaphore_wait(barrier, n)
+    send_pouch.start()
+    for step in reversed(range(half)):
+        dispatch(half + step).start()
+        if step > 0:
+            dispatch(step).start()
+    for share in shares:
+        share.start()
+    for slot in range(1, n):
+        send_flag(slot).start()
+
+    scores = lax.dot_general(
+        centroids_ref[...],
+        tokens_ref[...],
+        (((1,), (1,)), ((), ())),
+        preferred_element_type=jnp.float32,
+    )
+    experts = lax.broadcasted_iota(jnp.int32, scores.shape, 0)
+    chosen = jnp.sum(jnp.where(experts == ids, scores, 0.0), axis=0, keepdims=True)
+    gating = 1.0 / (1.0 + jnp.exp(-chosen))
+    which = lax.broadcasted_iota(jnp.int32, (128, tokens_here), 0)
+    columns[...] = jnp.where(which == 0, position.astype(jnp.float32), gating).T
+    slot_columns = lax.broadcasted_iota(jnp.int32, (tokens_here, direct_rows + spare), 1)
+    place[...] = (slot_columns == columns[:, 0:1].astype(jnp.int32)).astype(jnp.bfloat16)
+
+    def relay_out():
+        send_pouch.wait_recv()
+        opened = lax.dot_general(
+            inbox[:, width:],
+            inbox[:, :width],
+            (((0,), (0,)), ((), ())),
+            preferred_element_type=jnp.float32,
+        )
+        opened = opened[:far_rows].astype(jnp.bfloat16)
+        expanded[...] = opened
+        received[extra(0, direct_rows), :] = opened[:base]
+        for k in range(1, half):
+            forward(k).start()
+
+    def relay_home():
+        for k in range(1, half):
+            give_relay(k).wait_recv()
+            forward(k).wait_send()
+        closed = jnp.dot(
+            inbox[:, width : width + far_rows],
+            collected[...],
+            preferred_element_type=jnp.float32,
+        )
+        expanded[0:spare, :] = closed.astype(jnp.bfloat16)
+        back_pouch.start()
+
+    def multiply(here, part):
+        @pl.loop(0, pieces)
+        def _(piece):
+            cut = pl.ds(pl.multiple_of(piece * TILE, TILE), TILE)
+            middle = jnp.dot(
+                received[here, :], full_in[part, :, cut], preferred_element_type=jnp.float32
+            )
+            middle = jnp.maximum(middle, 0.0).astype(jnp.bfloat16)
+            total[...] += jnp.dot(
+                middle, full_out[part, cut, :], preferred_element_type=jnp.float32
+            )
+
+    ready = []
+
+    def chunk(which):
+        here = pl.ds(which * rows, rows)
+        if which == 3:
+            for k in range(1, half):
+                forward(k).wait_recv()
+        else:
+            first = which * half // 2 if which < 2 else half
+            count = half // 2 if which < 2 else half
+            for slot in range(first, first + count):
+                if slot > 0:
+                    dispatch(slot).wait_recv()
+        total[...] = jnp.zeros_like(total)
+        if not ready:
+            for load in loads:
+                load.wait()
+        multiply(here, 0)
+        if not ready:
+            for share in shares:
+                share.wait_recv()
+            ready.append(True)
+        multiply(here, 1)
+        done = total[...].astype(jnp.bfloat16)
+        result[here, :] = done
+        if which == 3:
+            collected[extra(0), :] = done[:base]
+            for k in range(1, half):
+                give_relay(k).start()
+        else:
+            for slot in range(first, first + count):
+                if slot > 0:
+                    give_back(slot).start()
+                else:
+                    returned[block(0), :] = done[:cap]
+
+    relay_out()
+    for which in ORDER:
+        if which == "home":
+            relay_home()
+        else:
+            chunk(which)
+
+    for slot in range(1, n):
+        send_flag(slot).wait_recv()
+    group = jnp.max(flags_in[...], axis=0)
+    group_out[...] = group
+    for slot in range(1, n):
+        send_flag(slot).wait_send()
+    swap_flag.start()
+
+    arrived = jnp.zeros((tokens_here, width), jnp.float32)
+    for which in FINISH:
+        if which == 3:
+            here = pl.ds(direct_rows, spare)
+            back_pouch.wait_recv()
+        else:
+            here = pl.ds(which * rows, rows)
+            first = which * half // 2 if which < 2 else half
+            count = half // 2 if which < 2 else half
+            for slot in range(first, first + count):
+                if slot > 0:
+                    give_back(slot).wait_recv()
+        arrived += jnp.dot(
+            place[:, here], returned[here, :], preferred_element_type=jnp.float32
+        )
+    mixed = tokens_ref[...].astype(jnp.float32) + columns[:, 1:2] * arrived
+    out_ref[...] = mixed.astype(jnp.bfloat16)
+
+    swap_flag.wait_recv()
+    spill_ref[0, 0] = jnp.max(jnp.maximum(group_out[...], group_in[...])).astype(jnp.int32)
+
+    swap_flag.wait_send()
+    send_pouch.wait_send()
+    back_pouch.wait_send()
+    for k in range(1, half):
+        give_relay(k).wait_send()
+    for slot in range(1, n):
+        dispatch(slot).wait_send()
+        give_back(slot).wait_send()
+    for share in shares:
+        share.wait_send()
+
+
+def with_relay(n, tokens, expert_ids, slot_ids, centroids, w_in, w_out):
+    count, width = tokens.shape
+    cap = 2 * count // n
+    half = n // 2
+    base = cap // 2
+    spare = cap + cap // 2
+    direct = half * (cap + base)
+    hidden = w_in.shape[2]
+    vmem = pl.BlockSpec(memory_space=pltpu.VMEM)
+    hbm = pl.BlockSpec(memory_space=pl.ANY)
+    sems = pltpu.SemaphoreType.DMA
+    bf16 = jnp.bfloat16
+    out, spill = pl.pallas_call(
+        functools.partial(relay_kernel, n, cap, spare),
+        out_shape=[
+            pltpu.VMEM((count, width), bf16),
+            jax.ShapeDtypeStruct((1, 1), jnp.int32),
+        ],
+        in_specs=[vmem, vmem, hbm, vmem, hbm, hbm],
+        out_specs=[vmem, pl.BlockSpec(memory_space=pltpu.SMEM)],
+        scratch_shapes=[
+            pltpu.VMEM((direct, width), bf16),
+            pltpu.VMEM((spare, width + 128), bf16),
+            pltpu.VMEM((spare, width + 128), bf16),
+            pltpu.VMEM((half * base, width), bf16),
+            pltpu.VMEM((n * cap, width), bf16),
+            pltpu.VMEM((n * cap, width), bf16),
+            pltpu.VMEM((half * base, width), bf16),
+            pltpu.VMEM((direct + spare, width), bf16),
+            pltpu.VMEM((half * cap // 2, width), jnp.float32),
+            pltpu.VMEM((count, width), bf16),
+            pltpu.VMEM((count, direct + spare), bf16),
+            pltpu.VMEM((count, 128), jnp.float32),
+            pltpu.VMEM((2, width, hidden), bf16),
+            pltpu.VMEM((2, hidden, width), bf16),
+            pltpu.VMEM((8, 128), jnp.float32),
+            pltpu.VMEM((n, 8, 128), jnp.float32),
+            pltpu.VMEM((8, 128), jnp.float32),
+            pltpu.VMEM((8, 128), jnp.float32),
+            sems((3,)),
+            sems((2,)),
+            sems((2,)),
+            sems((n,)),
+            sems((n,)),
+            sems((n,)),
+            sems((n,)),
+            sems((half,)),
+            sems((half,)),
+            sems((half,)),
+            sems((half,)),
+            sems((2,)),
+            sems((2,)),
+            sems((n,)),
+            sems((n,)),
+        ],
+        compiler_params=pltpu.CompilerParams(
+            collective_id=1, has_side_effects=True, vmem_limit_bytes=60 * 1024 * 1024
+        ),
+    )(
+        expert_ids.reshape(1, count),
+        slot_ids.reshape(1, count),
+        tokens,
+        centroids,
+        w_in,
+        w_out,
+    )
+    return lax.cond(
+        spill[0, 0] > 0,
+        lambda: in_one_kernel(n, tokens, expert_ids, slot_ids, centroids, w_in, w_out),
+        lambda: out,
+    )
+
+
 def in_plain_ops(tokens, expert_ids, slot_ids, centroids, w_in, w_out):
     experts = centroids.shape[0]
     count_rows = tokens.shape[0]
@@ -303,6 +738,9 @@
 
     def on_device(tokens, expert_ids, slot_ids, centroids, w_in, w_out):
         capacity = 2 * tokens.shape[0] // n
+        lanes_needed = (n // 2) * (capacity // 2)
+        if mesh.shape["grp"] == 2 and n % 4 == 0 and capacity % 32 == 0 and lanes_needed <= 128:
+            return with_relay(n, tokens, expert_ids, slot_ids, centroids, w_in, w_out)
         if mesh.shape["grp"] == 2 and n % 4 == 0 and capacity % 16 == 0:
             return in_one_kernel(n, tokens, expert_ids, slot_ids, centroids, w_in, w_out)
         return in_plain_ops(tokens, expert_ids, slot_ids, centroids, w_in, w_out)

time: 56.1 us -> 51.5 us (0.918)
  Pallas kernels: 55.1 us -> 49.3 us
  between operations: 0.01 us -> 0.74 us
    pallas_call x1, Pallas kernels: 55.1 us -> 49.3 us  [with_relay(): pl.pallas_call(functools.partial(relay_kernel, n, cap, spare), out_shape=...]
where the time goes in v1:
time: 51.5 us; the launch traced here: 50.8 us
  Pallas kernels  49.3 us (96%)
  local copies, waits for them, and re-layouts  0.81 us (2%)
  between operations  0.74 us (1%)
    pallas_call x1, Pallas kernels, with_relay(): pl.pallas_call(functools.partial(relay_kernel, n, cap, spare), out_shape=...  49.3 us

profile of v1, /device:TPU:0, one launch (start us, length us, event | category | flops | bytes accessed | tf_op | source)
XLA Modules:
  0.0 50.8 jit_solution(6427003080320949159)
XLA Ops:
  0.0 0.0 copy-start
  0.0 0.0 copy-start.1
  0.0 0.0 copy-start.2
  0.0 0.0 copy-start.3
  0.0 49.3 %shard_map.66 = (bf16[256,1024]{1,0:T(8,128)(2,1)S(1)}, s32[1,1]{1,0:T(1,128)}) custom-call(s32[1,256]{1,0:T(1,128)} %bitcast.5, s32[1,256]{1,0:T(1,128)} %bitcast.7, bf16[256,1024]{1,0:T(8,128)(2,1)} %tokens_hbm.1, bf16[16,1024]{1,0:T(8,128)(2,1)} %centroids_ref.1, bf16[1,1024,2048]{2,1,0:T(8,128)(2,1)} %w_in_ref.1, bf16[1,2048,1024]{2,1,0:T(8,128)(2,1)} %w_out_ref.1), custom_call_target="tpu_custom_call" | custom-call | tf_op jit(solution)/shard_map/pallas_call | solution.py:639
  50.0 0.0 copy-done
  50.0 0.0 copy-done.1
  50.0 0.0 copy-done.2
  50.0 0.0 copy-done.3
  50.0 0.8 %copy.12 = bf16[256,1024]{1,0:T(8,128)(2,1)} copy(bf16[256,1024]{1,0:T(8,128)(2,1)S(1)} %get-tuple-element.31) | data formatting | bytes 1048576
  (1 shorter events, 0.0 us)
Async XLA Ops:
  0.0 50.0 %copy-start = (bf16[256,1024]{1,0:T(8,128)(2,1)S(1)}, bf16[256,1024]{1,0:T(8,128)(2,1)}, u32[]{:S(2)}) copy-start(bf16[256,1024]{1,0:T(8,128)(2,1)} %tokens_hbm.1) | copy-start | bytes 1572868
  0.0 50.0 %copy-start.1 = (bf16[16,1024]{1,0:T(8,128)(2,1)S(1)}, bf16[16,1024]{1,0:T(8,128)(2,1)}, u32[]{:S(2)}) copy-start(bf16[16,1024]{1,0:T(8,128)(2,1)} %centroids_ref.1) | copy-start | bytes 98308
  0.0 50.0 %copy-start.2 = (s32[256]{0:T(256)S(1)}, s32[256]{0:T(256)}, u32[]{:S(2)}) copy-start(s32[256]{0:T(256)} %param.9) | copy-start | bytes 3076
  0.0 50.0 %copy-start.3 = (s32[256]{0:T(256)S(1)}, s32[256]{0:T(256)}, u32[]{:S(2)}) copy-start(s32[256]{0:T(256)} %param.10) | copy-start | bytes 3076

commit v2 on v1

--- a/solution.py
+++ b/solution.py
@@ -9,8 +9,8 @@
 
 MESH = pl.DeviceIdType.MESH
 TILE = 1024
-ORDER = (1, 3, 2, "home", 0)
-FINISH = (1, 2, 0, 3)
+PLAN = ('pouch', 1, 2, 3, 8, 'settle', 'most', 9, 10, 11, 4, 5, 6, 7, 'relay', 'all', 12, 13, 14, 15, 'flags', 'n0', 'fa', 'n1', 'relayed', 'share', 'fb', 'drain', 'home')
+FINISH = ('n0', 'n1', 'spill', 'fa', 'fb', 'pouch')
 
 
 def expert_kernel(
@@ -268,14 +268,18 @@
     n,
     cap,
     spare,
-    ids_ref,
-    slots_ref,
+    ids_hbm,
+    slots_hbm,
     tokens_hbm,
-    centroids_ref,
+    centroids_hbm,
     w_in_ref,
     w_out_ref,
     out_ref,
-    spill_ref,
+    spill_hbm,
+    ids_ref,
+    slots_ref,
+    tokens_ref,
+    centroids_ref,
     outgoing,
     pouch,
     inbox,
@@ -284,8 +288,6 @@
     result,
     collected,
     returned,
-    total,
-    tokens_ref,
     place,
     columns,
     full_in,
@@ -294,6 +296,7 @@
     flags_in,
     group_out,
     group_in,
+    spill_ref,
     load_sem,
     share_send,
     share_recv,
@@ -309,32 +312,38 @@
     pouch_recv,
     flag_send,
     flag_recv,
+    rounds,
+    gates,
 ):
     grp = lax.axis_index("grp")
     me = lax.axis_index("ex")
     half = n // 2
+    plane = n // 4
     base = cap // 2
-    side = me // half
-    seat = me % half
-    mirror = (1 - side) * half + seat
     near_rows = half * cap
     far_rows = half * base
     direct_rows = near_rows + far_rows
-    rows = near_rows // 2
     tokens_here, width = tokens_ref.shape
     hidden = full_in.shape[2]
     pieces = hidden // TILE
-
-    def peer_to(slot):
-        return ((side + slot // half) % 2) * half + (seat + slot % half) % half
-
-    def peer_from(slot):
-        return ((side + slot // half) % 2) * half + (seat + half - slot % half) % half
+    partner = {"grp": 1 - grp}
+
+    def peer(slot):
+        where = me
+        bit = 1
+        while bit < n:
+            if slot & bit:
+                where = where + bit - 2 * bit * ((me // bit) % 2)
+            bit *= 2
+        return where
+
+    def rows_of(slot):
+        if slot < half:
+            return slot * cap, cap
+        return near_rows + (slot - half) * base, base
 
     def block(slot):
-        if slot < half:
-            return pl.ds(slot * cap, cap)
-        return pl.ds(near_rows + (slot - half) * base, base)
+        return pl.ds(*rows_of(slot))
 
     def extra(k, start=0):
         return pl.ds(start + k * base, base)
@@ -355,7 +364,7 @@
             received.at[block(slot), :],
             send_sem.at[slot],
             recv_sem.at[slot],
-            {"ex": peer_to(slot)},
+            {"ex": peer(slot)},
         )
 
     def give_back(slot):
@@ -364,7 +373,7 @@
             returned.at[block(slot), :],
             back_send.at[slot],
             back_recv.at[slot],
-            {"ex": peer_from(slot)},
+            {"ex": peer(slot)},
         )
 
     def forward(k):
@@ -373,7 +382,7 @@
             received.at[extra(k, direct_rows), :],
             relay_send.at[k],
             relay_recv.at[k],
-            {"ex": peer_to(k)},
+            {"ex": peer(k)},
         )
 
     def give_relay(k):
@@ -382,47 +391,116 @@
             collected.at[extra(k), :],
             relay_back_send.at[k],
             relay_back_recv.at[k],
-            {"ex": peer_from(k)},
-        )
-
-    send_pouch = remote(pouch, inbox, pouch_send.at[0], pouch_recv.at[0], {"ex": mirror})
+            {"ex": peer(k)},
+        )
+
+    send_pouch = remote(pouch, inbox, pouch_send.at[0], pouch_recv.at[0], {"ex": peer(half)})
     back_pouch = remote(
         expanded.at[pl.ds(0, spare), :],
         returned.at[pl.ds(direct_rows, spare), :],
         pouch_send.at[1],
         pouch_recv.at[1],
-        {"ex": mirror},
+        {"ex": peer(half)},
     )
 
     def send_flag(slot):
         return remote(
-            flag_out, flags_in.at[slot], flag_send.at[slot], flag_recv.at[slot], {"ex": peer_to(slot)}
-        )
-
-    swap_flag = remote(group_out, group_in, flag_send.at[0], flag_recv.at[0], {"grp": 1 - grp})
+            flag_out, flags_in.at[slot], flag_send.at[slot], flag_recv.at[slot], {"ex": peer(slot)}
+        )
+
+    swap_flag = remote(group_out, group_in, flag_send.at[0], flag_recv.at[0], partner)
+
+    small = [
+        pltpu.make_async_copy(ids_hbm, ids_ref, load_sem.at[0]),
+        pltpu.make_async_copy(slots_hbm, slots_ref, load_sem.at[1]),
+        pltpu.make_async_copy(tokens_hbm, tokens_ref, load_sem.at[2]),
+        pltpu.make_async_copy(centroids_hbm, centroids_ref, load_sem.at[3]),
+    ]
+    loads = [
+        pltpu.make_async_copy(w_in_ref.at[0], full_in.at[0], load_sem.at[4]),
+        pltpu.make_async_copy(w_out_ref.at[0], full_out.at[0], load_sem.at[5]),
+    ]
+    shares = []
+    for piece in range(pieces):
+        cut = pl.ds(piece * TILE, TILE)
+        first = remote(
+            w_in_ref.at[0, :, cut],
+            full_in.at[1, :, cut],
+            share_send.at[0, piece],
+            share_recv.at[0, piece],
+            partner,
+        )
+        second = remote(
+            w_out_ref.at[0, cut, :],
+            full_out.at[1, cut, :],
+            share_send.at[1, piece],
+            share_recv.at[1, piece],
+            partner,
+        )
+        shares.append((first, second))
 
     barrier = pltpu.get_barrier_semaphore()
-    for slot in range(1, n):
-        pl.semaphore_signal(
-            barrier, inc=1, device_id={"ex": peer_to(slot)}, device_id_type=MESH
-        )
-    pl.semaphore_signal(barrier, inc=1, device_id={"grp": 1 - grp}, device_id_type=MESH)
-
-    bring = pltpu.make_async_copy(tokens_hbm, tokens_ref, load_sem.at[2])
-    bring.start()
-    loads = [
-        pltpu.make_async_copy(w_in_ref.at[0], full_in.at[0], load_sem.at[0]),
-        pltpu.make_async_copy(w_out_ref.at[0], full_out.at[0], load_sem.at[1]),
-    ]
+    level = me // plane
+
+    def near_masks(reach):
+        return [mask for mask in range(plane) if mask.bit_count() <= reach]
+
+    def call(sem, reach):
+        def ring(where):
+            pl.semaphore_signal(sem, inc=1, device_id={"ex": where}, device_id_type=MESH)
+
+        for mask in near_masks(reach):
+            if mask > 0:
+                ring(peer(mask))
+        for step in range(1, reach + 1):
+
+            @pl.when(level + step < 4)
+            def _():
+                for mask in near_masks(reach - step):
+                    ring(peer(mask) + step * plane)
+
+            @pl.when(level >= step)
+            def _():
+                for mask in near_masks(reach - step):
+                    ring(peer(mask) - step * plane)
+
+    def answer(sem, reach):
+        count = jnp.int32(len(near_masks(reach)) - 1)
+        for step in range(1, reach + 1):
+            masks = len(near_masks(reach - step))
+            count += masks * (level + step < 4).astype(jnp.int32)
+            count += masks * (level >= step).astype(jnp.int32)
+        pl.semaphore_wait(sem, count)
+
+    def release(gate):
+        pl.semaphore_signal(gates.at[gate], inc=1, device_id=partner, device_id_type=MESH)
+
+    for load in small:
+        load.start()
+
+    @pl.when(grp == 0)
+    def _():
+        pl.semaphore_wait(barrier, 1)
+        pl.semaphore_signal(gates.at[0], inc=1, device_id=partner, device_id_type=MESH)
+
+    @pl.when(grp == 1)
+    def _():
+        pl.semaphore_signal(barrier, inc=1, device_id=partner, device_id_type=MESH)
+        pl.semaphore_wait(gates.at[0], 1)
+        call(barrier, 2)
+
     for load in loads:
         load.start()
-
+    for pair in shares:
+        for share in pair:
+            share.start()
+
+    small[0].wait()
+    small[1].wait()
     ids = ids_ref[...]
     slots = slots_ref[...]
-    high = (ids >= half).astype(jnp.int32)
-    ahead = ids - high * half - seat
-    ahead = jnp.where(ahead < 0, ahead + half, ahead)
-    across = high != side
+    offset = jnp.bitwise_xor(ids, me)
+    across = offset >= half
     order = (ids * cap + slots).astype(jnp.float32)
     floor = (ids * cap).astype(jnp.float32)
     columns[...] = jnp.broadcast_to(order, (128, tokens_here)).T
@@ -439,8 +517,8 @@
     queue = queue.astype(jnp.int32)
     position = jnp.where(
         across,
-        jnp.where(late, direct_rows + queue, near_rows + ahead * base + rank),
-        ahead * cap + slots,
+        jnp.where(late, direct_rows + queue, near_rows + (offset - half) * base + rank),
+        offset * cap + slots,
     )
     spill = jnp.max(jnp.where(late, queue + 1, 0), axis=1, keepdims=True) > spare
     flag_out[...] = jnp.broadcast_to(jnp.where(spill, 1.0, 0.0), flag_out.shape)
@@ -449,58 +527,55 @@
     slot_rows = lax.broadcasted_iota(jnp.int32, (direct_rows + spare, tokens_here), 0)
     hits = slot_rows == position
     spread = hits.astype(jnp.bfloat16)
-    target = (ahead * base + rank - base + 1).astype(jnp.float32)
+    target = ((offset - half) * base + rank - base + 1).astype(jnp.float32)
     aim = jnp.sum(jnp.where(hits[direct_rows:], target, 0.0), axis=1, keepdims=True)
     wide = lax.broadcasted_iota(jnp.int32, (spare, 128), 1).astype(jnp.float32)
     pouch[:, width:] = (wide == aim - 1.0).astype(jnp.bfloat16)
-    bring.wait()
+    small[2].wait()
     packed = jnp.dot(spread, tokens_ref[...], preferred_element_type=jnp.float32)
     packed = packed.astype(jnp.bfloat16)
+    pouch[:, :width] = packed[direct_rows:]
     outgoing[...] = packed[:direct_rows]
-    pouch[:, :width] = packed[direct_rows:]
     received[block(0), :] = packed[:cap]
 
-    shares = [
-        remote(
-            w_in_ref.at[0],
-            full_in.at[1],
-            share_send.at[0],
-            share_recv.at[0],
-            {"grp": 1 - grp},
-        ),
-        remote(
-            w_out_ref.at[0],
-            full_out.at[1],
-            share_send.at[1],
-            share_recv.at[1],
-            {"grp": 1 - grp},
-        ),
-    ]
-
-    pl.semaphore_wait(barrier, n)
-    send_pouch.start()
-    for step in reversed(range(half)):
-        dispatch(half + step).start()
-        if step > 0:
-            dispatch(step).start()
-    for share in shares:
-        share.start()
-    for slot in range(1, n):
-        send_flag(slot).start()
-
-    scores = lax.dot_general(
-        centroids_ref[...],
-        tokens_ref[...],
-        (((1,), (1,)), ((), ())),
-        preferred_element_type=jnp.float32,
-    )
-    experts = lax.broadcasted_iota(jnp.int32, scores.shape, 0)
-    chosen = jnp.sum(jnp.where(experts == ids, scores, 0.0), axis=0, keepdims=True)
-    gating = 1.0 / (1.0 + jnp.exp(-chosen))
-    which = lax.broadcasted_iota(jnp.int32, (128, tokens_here), 0)
-    columns[...] = jnp.where(which == 0, position.astype(jnp.float32), gating).T
-    slot_columns = lax.broadcasted_iota(jnp.int32, (tokens_here, direct_rows + spare), 1)
-    place[...] = (slot_columns == columns[:, 0:1].astype(jnp.int32)).astype(jnp.bfloat16)
+    @pl.when(grp == 1)
+    def _():
+        answer(barrier, 2)
+        release(1)
+        call(rounds.at[0], 2)
+
+    @pl.when(grp == 0)
+    def _():
+        pl.semaphore_wait(gates.at[1], 1)
+
+    def settle():
+        small[3].wait()
+        scores = lax.dot_general(
+            centroids_ref[...],
+            tokens_ref[...],
+            (((1,), (1,)), ((), ())),
+            preferred_element_type=jnp.float32,
+        )
+        experts = lax.broadcasted_iota(jnp.int32, scores.shape, 0)
+        chosen = jnp.sum(jnp.where(experts == ids, scores, 0.0), axis=0, keepdims=True)
+        gating = 1.0 / (1.0 + jnp.exp(-chosen))
+        which = lax.broadcasted_iota(jnp.int32, (128, tokens_here), 0)
+        columns[...] = jnp.where(which == 0, position.astype(jnp.float32), gating).T
+        slot_columns = lax.broadcasted_iota(jnp.int32, (tokens_here, direct_rows + spare), 1)
+        own = columns[:, 0:1].astype(jnp.int32)
+        place[...] = (slot_columns == own).astype(jnp.bfloat16)
+
+    def gate(number):
+        @pl.when(grp == 1)
+        def _():
+            answer(rounds.at[number - 2], 2 if number == 2 else 1)
+            release(number)
+            if number == 2:
+                call(rounds.at[1], 1)
+
+        @pl.when(grp == 0)
+        def _():
+            pl.semaphore_wait(gates.at[number], 1)
 
     def relay_out():
         send_pouch.wait_recv()
@@ -515,6 +590,10 @@
         received[extra(0, direct_rows), :] = opened[:base]
         for k in range(1, half):
             forward(k).start()
+
+    def send_flags():
+        for slot in range(1, n):
+            send_flag(slot).start()
 
     def relay_home():
         for k in range(1, half):
@@ -528,100 +607,126 @@
         expanded[0:spare, :] = closed.astype(jnp.bfloat16)
         back_pouch.start()
 
-    def multiply(here, part):
-        @pl.loop(0, pieces)
-        def _(piece):
-            cut = pl.ds(pl.multiple_of(piece * TILE, TILE), TILE)
-            middle = jnp.dot(
-                received[here, :], full_in[part, :, cut], preferred_element_type=jnp.float32
-            )
-            middle = jnp.maximum(middle, 0.0).astype(jnp.bfloat16)
-            total[...] += jnp.dot(
-                middle, full_out[part, cut, :], preferred_element_type=jnp.float32
-            )
-
     ready = []
 
-    def chunk(which):
-        here = pl.ds(which * rows, rows)
-        if which == 3:
-            for k in range(1, half):
-                forward(k).wait_recv()
-        else:
-            first = which * half // 2 if which < 2 else half
-            count = half // 2 if which < 2 else half
-            for slot in range(first, first + count):
-                if slot > 0:
-                    dispatch(slot).wait_recv()
-        total[...] = jnp.zeros_like(total)
-        if not ready:
+    def expert(start, count):
+        here = pl.ds(start, count)
+        fresh = not ready
+        ready.append(True)
+        if fresh:
             for load in loads:
                 load.wait()
-        multiply(here, 0)
-        if not ready:
-            for share in shares:
-                share.wait_recv()
-            ready.append(True)
-        multiply(here, 1)
-        done = total[...].astype(jnp.bfloat16)
+        done = None
+        for part in range(2):
+            for piece in range(pieces):
+                if fresh and part == 1:
+                    for share in shares[piece]:
+                        share.wait_recv()
+                cut = pl.ds(piece * TILE, TILE)
+                middle = jnp.dot(
+                    received[here, :], full_in[part, :, cut], preferred_element_type=jnp.float32
+                )
+                middle = jnp.maximum(middle, 0.0).astype(jnp.bfloat16)
+                more = jnp.dot(middle, full_out[part, cut, :], preferred_element_type=jnp.float32)
+                done = more if done is None else done + more
+        done = done.astype(jnp.bfloat16)
         result[here, :] = done
-        if which == 3:
-            collected[extra(0), :] = done[:base]
-            for k in range(1, half):
-                give_relay(k).start()
+        return done
+
+    def direct_chunk(chosen_slots):
+        for slot in chosen_slots:
+            if slot > 0:
+                dispatch(slot).wait_recv()
+        start = rows_of(chosen_slots[0])[0]
+        done = expert(start, sum(rows_of(slot)[1] for slot in chosen_slots))
+        for slot in chosen_slots:
+            if slot > 0:
+                give_back(slot).start()
+            else:
+                returned[block(0), :] = done[:cap]
+
+    def share_flags():
+        for slot in range(1, n):
+            send_flag(slot).wait_recv()
+        group_out[...] = jnp.max(flags_in[...], axis=0)
+        for slot in range(1, n):
+            send_flag(slot).wait_send()
+        swap_flag.start()
+
+    def drain():
+        send_pouch.wait_send()
+        for slot in range(1, n):
+            dispatch(slot).wait_send()
+        for pair in shares:
+            for share in pair:
+                share.wait_send()
+
+    def relayed_chunk():
+        for k in range(1, half):
+            forward(k).wait_recv()
+        done = expert(direct_rows, far_rows)
+        collected[extra(0), :] = done[:base]
+        for k in range(1, half):
+            give_relay(k).start()
+
+    groups = {
+        "n0": range(0, plane),
+        "n1": range(plane, half),
+        "fa": range(half, half + plane),
+        "fb": range(half + plane, n),
+    }
+    steps = {
+        "pouch": send_pouch.start,
+        "settle": settle,
+        "most": lambda: gate(2),
+        "all": lambda: gate(3),
+        "relay": relay_out,
+        "flags": send_flags,
+        "relayed": relayed_chunk,
+        "home": relay_home,
+        "share": share_flags,
+        "drain": drain,
+    }
+    for step in PLAN:
+        if step in steps:
+            steps[step]()
+        elif step in groups:
+            direct_chunk(groups[step])
         else:
-            for slot in range(first, first + count):
-                if slot > 0:
-                    give_back(slot).start()
-                else:
-                    returned[block(0), :] = done[:cap]
-
-    relay_out()
-    for which in ORDER:
-        if which == "home":
-            relay_home()
-        else:
-            chunk(which)
-
-    for slot in range(1, n):
-        send_flag(slot).wait_recv()
-    group = jnp.max(flags_in[...], axis=0)
-    group_out[...] = group
-    for slot in range(1, n):
-        send_flag(slot).wait_send()
-    swap_flag.start()
+            dispatch(step).start()
 
     arrived = jnp.zeros((tokens_here, width), jnp.float32)
-    for which in FINISH:
-        if which == 3:
+    for name in FINISH:
+        if name == "spill":
+            swap_flag.wait_recv()
+            worst = jnp.max(jnp.maximum(group_out[...], group_in[...]))
+            spill_ref[0, 0] = worst.astype(jnp.int32)
+            tell = pltpu.make_async_copy(spill_ref, spill_hbm, load_sem.at[0])
+            tell.start()
+            swap_flag.wait_send()
+            continue
+        if name == "pouch":
             here = pl.ds(direct_rows, spare)
             back_pouch.wait_recv()
         else:
-            here = pl.ds(which * rows, rows)
-            first = which * half // 2 if which < 2 else half
-            count = half // 2 if which < 2 else half
-            for slot in range(first, first + count):
+            for slot in groups[name]:
                 if slot > 0:
                     give_back(slot).wait_recv()
+            here = pl.ds(
+                rows_of(groups[name][0])[0], sum(rows_of(slot)[1] for slot in groups[name])
+            )
         arrived += jnp.dot(
             place[:, here], returned[here, :], preferred_element_type=jnp.float32
         )
-    mixed = tokens_ref[...].astype(jnp.float32) + columns[:, 1:2] * arrived
-    out_ref[...] = mixed.astype(jnp.bfloat16)
-
-    swap_flag.wait_recv()
-    spill_ref[0, 0] = jnp.max(jnp.maximum(group_out[...], group_in[...])).astype(jnp.int32)
-
-    swap_flag.wait_send()
-    send_pouch.wait_send()
+    sums = tokens_ref[...].astype(jnp.float32) + columns[:, 1:2] * arrived
+    out_ref[...] = sums.astype(jnp.bfloat16)
+
     back_pouch.wait_send()
     for k in range(1, half):
         give_relay(k).wait_send()
     for slot in range(1, n):
-        dispatch(slot).wait_send()
         give_back(slot).wait_send()
-    for share in shares:
-        share.wait_send()
+    tell.wait()
 
 
 def with_relay(n, tokens, expert_ids, slot_ids, centroids, w_in, w_out):
@@ -632,9 +737,9 @@
     spare = cap + cap // 2
     direct = half * (cap + base)
     hidden = w_in.shape[2]
-    vmem = pl.BlockSpec(memory_space=pltpu.VMEM)
     hbm = pl.BlockSpec(memory_space=pl.ANY)
     sems = pltpu.SemaphoreType.DMA
+    flags = pltpu.SemaphoreType.REGULAR
     bf16 = jnp.bfloat16
     out, spill = pl.pallas_call(
         functools.partial(relay_kernel, n, cap, spare),
@@ -642,9 +747,13 @@
             pltpu.VMEM((count, width), bf16),
             jax.ShapeDtypeStruct((1, 1), jnp.int32),
         ],
-        in_specs=[vmem, vmem, hbm, vmem, hbm, hbm],
-        out_specs=[vmem, pl.BlockSpec(memory_space=pltpu.SMEM)],
+        in_specs=[hbm] * 6,
+        out_specs=[pl.BlockSpec(memory_space=pltpu.VMEM), hbm],
         scratch_shapes=[
+            pltpu.VMEM((1, count), jnp.int32),
+            pltpu.VMEM((1, count), jnp.int32),
+            pltpu.VMEM((count, width), bf16),
+            pltpu.VMEM(centroids.shape, bf16),
             pltpu.VMEM((direct, width), bf16),
             pltpu.VMEM((spare, width + 128), bf16),
             pltpu.VMEM((spare, width + 128), bf16),
@@ -653,8 +762,6 @@
             pltpu.VMEM((n * cap, width), bf16),
             pltpu.VMEM((half * base, width), bf16),
             pltpu.VMEM((direct + spare, width), bf16),
-            pltpu.VMEM((half * cap // 2, width), jnp.float32),
-            pltpu.VMEM((count, width), bf16),
             pltpu.VMEM((count, direct + spare), bf16),
             pltpu.VMEM((count, 128), jnp.float32),
             pltpu.VMEM((2, width, hidden), bf16),
@@ -663,9 +770,10 @@
             pltpu.VMEM((n, 8, 128), jnp.float32),
             pltpu.VMEM((8, 128), jnp.float32),
             pltpu.VMEM((8, 128), jnp.float32),
-            sems((3,)),
-            sems((2,)),
-            sems((2,)),
+            pltpu.SMEM((1, 1), jnp.int32),
+            sems((6,)),
+            sems((2, hidden // TILE)),
+            sems((2, hidden // TILE)),
             sems((n,)),
             sems((n,)),
             sems((n,)),
@@ -678,6 +786,8 @@
             sems((2,)),
             sems((n,)),
             sems((n,)),
+            flags((2,)),
+            flags((4,)),
         ],
         compiler_params=pltpu.CompilerParams(
             collective_id=1, has_side_effects=True, vmem_limit_bytes=60 * 1024 * 1024
@@ -690,10 +800,12 @@
         w_in,
         w_out,
     )
-    return lax.cond(
-        spill[0, 0] > 0,
-        lambda: in_one_kernel(n, tokens, expert_ids, slot_ids, centroids, w_in, w_out),
-        lambda: out,
+    return lax.switch(
+        spill[0, 0],
+        [
+            lambda: out,
+            lambda: in_one_kernel(n, tokens, expert_ids, slot_ids, centroids, w_in, w_out),
+        ],
     )
 
 
@@ -739,7 +851,7 @@
     def on_device(tokens, expert_ids, slot_ids, centroids, w_in, w_out):
         capacity = 2 * tokens.shape[0] // n
         lanes_needed = (n // 2) * (capacity // 2)
-        if mesh.shape["grp"] == 2 and n % 4 == 0 and capacity % 32 == 0 and lanes_needed <= 128:
+        if mesh.shape["grp"] == 2 and n >= 8 and n & (n - 1) == 0 and capacity % 32 == 0 and lanes_needed <= 128:
             return with_relay(n, tokens, expert_ids, slot_ids, centroids, w_in, w_out)
         if mesh.shape["grp"] == 2 and n % 4 == 0 and capacity % 16 == 0:
             return in_one_kernel(n, tokens, expert_ids, slot_ids, centroids, w_in, w_out)

time: 51.5 us -> 47.4 us (0.920)
  Pallas kernels: 49.3 us -> 45.3 us
    pallas_call x1, Pallas kernels: 49.3 us -> 45.3 us  [with_relay(): pl.pallas_call(functools.partial(relay_kernel, n, cap, spare), out_shape=...]
where the time goes in v2:
time: 47.4 us; the launch traced here: 46.8 us
  Pallas kernels  45.3 us (96%)
  local copies, waits for them, and re-layouts  0.81 us (2%)
  between operations  0.74 us (2%)
    pallas_call x1, Pallas kernels, with_relay(): pl.pallas_call(functools.partial(relay_kernel, n, cap, spare), out_shape=...  45.3 us

profile of v2, /device:TPU:0, one launch (start us, length us, event | category | flops | bytes accessed | tf_op | source)
XLA Modules:
  0.0 46.8 jit_solution(10394651474437815694)
XLA Ops:
  0.0 0.0 copy-start
  0.0 0.0 copy-start.1
  0.0 0.0 copy-start.2
  0.0 0.0 copy-start.3
  0.0 45.3 %shard_map.66 = (bf16[256,1024]{1,0:T(8,128)(2,1)S(1)}, s32[1,1]{1,0:T(1,128)}) custom-call(s32[1,256]{1,0:T(1,128)} %bitcast.5, s32[1,256]{1,0:T(1,128)} %bitcast.7, bf16[256,1024]{1,0:T(8,128)(2,1)} %tokens_hbm.1, bf16[16,1024]{1,0:T(8,128)(2,1)} %centroids_hbm.1, bf16[1,1024,2048]{2,1,0:T(8,128)(2,1)} %w_in_ref.1, bf16[1,2048,1024]{2,1,0:T(8,128)(2,1)} %w_out_ref.1), custom_call_target="tpu_custom_call" | custom-call | tf_op jit(solution)/shard_map/pallas_call | solution.py:744
  46.0 0.0 copy-done
  46.0 0.0 copy-done.1
  46.0 0.0 copy-done.2
  46.0 0.0 copy-done.3
  46.0 0.8 %copy.12 = bf16[256,1024]{1,0:T(8,128)(2,1)} copy(bf16[256,1024]{1,0:T(8,128)(2,1)S(1)} %get-tuple-element.31) | data formatting | bytes 1048576
  (1 shorter events, 0.0 us)
Async XLA Ops:
  0.0 46.0 %copy-start = (bf16[256,1024]{1,0:T(8,128)(2,1)S(1)}, bf16[256,1024]{1,0:T(8,128)(2,1)}, u32[]{:S(2)}) copy-start(bf16[256,1024]{1,0:T(8,128)(2,1)} %tokens_hbm.1) | copy-start | bytes 1572868
  0.0 46.0 %copy-start.1 = (bf16[16,1024]{1,0:T(8,128)(2,1)S(1)}, bf16[16,1024]{1,0:T(8,128)(2,1)}, u32[]{:S(2)}) copy-start(bf16[16,1024]{1,0:T(8,128)(2,1)} %centroids_hbm.1) | copy-start | bytes 98308
  0.0 46.0 %copy-start.2 = (s32[256]{0:T(256)S(1)}, s32[256]{0:T(256)}, u32[]{:S(2)}) copy-start(s32[256]{0:T(256)} %param.9) | copy-start | bytes 3076
  0.0 46.0 %copy-start.3 = (s32[256]{0:T(256)S(1)}, s32[256]{0:T(256)}, u32[]{:S(2)}) copy-start(s32[256]{0:T(256)} %param.10) | copy-start | bytes 3076

commit v3 on v2

--- a/solution.py
+++ b/solution.py
@@ -9,8 +9,8 @@
 
 MESH = pl.DeviceIdType.MESH
 TILE = 1024
-PLAN = ('pouch', 1, 2, 3, 8, 'settle', 'most', 9, 10, 11, 4, 5, 6, 7, 'relay', 'all', 12, 13, 14, 15, 'flags', 'n0', 'fa', 'n1', 'relayed', 'share', 'fb', 'drain', 'home')
-FINISH = ('n0', 'n1', 'spill', 'fa', 'fb', 'pouch')
+PLAN = ('pouch', 1, 2, 3, 8, 'settle', 'most', 9, 10, 11, 4, 5, 6, 7, 'relay', 'all', 12, 13, 14, 15, 'flags', 'n0', 'fa', 'n1', 'relayed', 'fb', 'drain', 'home', 'share')
+FINISH = ('n0', 'n1', 'fa', 'fb', 'spill', 'pouch')
 
 
 def expert_kernel(
@@ -362,8 +362,8 @@
         return remote(
             outgoing.at[block(slot), :],
             received.at[block(slot), :],
-            send_sem.at[slot],
-            recv_sem.at[slot],
+            send_sem.at[0],
+            recv_sem.at[slot // plane],
             {"ex": peer(slot)},
         )
 
@@ -371,8 +371,8 @@
         return remote(
             result.at[block(slot), :],
             returned.at[block(slot), :],
-            back_send.at[slot],
-            back_recv.at[slot],
+            back_send.at[0],
+            back_recv.at[slot // plane],
             {"ex": peer(slot)},
         )
 
@@ -380,8 +380,8 @@
         return remote(
             expanded.at[extra(k), :],
             received.at[extra(k, direct_rows), :],
-            relay_send.at[k],
-            relay_recv.at[k],
+            relay_send.at[0],
+            relay_recv.at[0],
             {"ex": peer(k)},
         )
 
@@ -389,8 +389,8 @@
         return remote(
             result.at[extra(k, direct_rows), :],
             collected.at[extra(k), :],
-            relay_back_send.at[k],
-            relay_back_recv.at[k],
+            relay_back_send.at[0],
+            relay_back_recv.at[0],
             {"ex": peer(k)},
         )
 
@@ -405,8 +405,57 @@
 
     def send_flag(slot):
         return remote(
-            flag_out, flags_in.at[slot], flag_send.at[slot], flag_recv.at[slot], {"ex": peer(slot)}
-        )
+            flag_out, flags_in.at[slot], flag_send.at[1], flag_recv.at[1], {"ex": peer(slot)}
+        )
+
+    def rows_in_all(first, last):
+        start = rows_of(first)[0]
+        return pl.ds(start, sum(rows_of(slot)[1] for slot in range(first, last)))
+
+    def many(src, dst, send, recv, first, last):
+        here = rows_in_all(first, last)
+        return remote(src.at[here, :], dst.at[here, :], send, recv, {"ex": peer(1)})
+
+    def all_sent():
+        return many(outgoing, received, send_sem.at[0], recv_sem.at[0], 1, n)
+
+    def all_given():
+        return many(result, returned, back_send.at[0], back_recv.at[0], 1, n)
+
+    def landed(group):
+        first = max(group * plane, 1)
+        return many(
+            outgoing, received, send_sem.at[0], recv_sem.at[group], first, (group + 1) * plane
+        )
+
+    def came_back(group):
+        first = max(group * plane, 1)
+        return many(
+            result, returned, back_send.at[0], back_recv.at[group], first, (group + 1) * plane
+        )
+
+    others = pl.ds(base, far_rows - base)
+    all_forward = remote(
+        expanded.at[others, :],
+        received.at[pl.ds(direct_rows + base, far_rows - base), :],
+        relay_send.at[0],
+        relay_recv.at[0],
+        {"ex": peer(1)},
+    )
+    all_relay = remote(
+        result.at[pl.ds(direct_rows + base, far_rows - base), :],
+        collected.at[others, :],
+        relay_back_send.at[0],
+        relay_back_recv.at[0],
+        {"ex": peer(1)},
+    )
+    all_flags = remote(
+        flags_in.at[pl.ds(1, n - 1)],
+        flags_in.at[pl.ds(1, n - 1)],
+        flag_send.at[1],
+        flag_recv.at[1],
+        {"ex": peer(1)},
+    )
 
     swap_flag = remote(group_out, group_in, flag_send.at[0], flag_recv.at[0], partner)
 
@@ -426,18 +475,22 @@
         first = remote(
             w_in_ref.at[0, :, cut],
             full_in.at[1, :, cut],
-            share_send.at[0, piece],
+            share_send.at[0],
             share_recv.at[0, piece],
             partner,
         )
         second = remote(
             w_out_ref.at[0, cut, :],
             full_out.at[1, cut, :],
-            share_send.at[1, piece],
+            share_send.at[1],
             share_recv.at[1, piece],
             partner,
         )
         shares.append((first, second))
+    sent_in = remote(w_in_ref.at[0], full_in.at[1], share_send.at[0], share_recv.at[0, 0], partner)
+    sent_out = remote(
+        w_out_ref.at[0], full_out.at[1], share_send.at[1], share_recv.at[1, 0], partner
+    )
 
     barrier = pltpu.get_barrier_semaphore()
     level = me // plane
@@ -588,7 +641,7 @@
         opened = opened[:far_rows].astype(jnp.bfloat16)
         expanded[...] = opened
         received[extra(0, direct_rows), :] = opened[:base]
-        for k in range(1, half):
+        for k in reversed(range(1, half)):
             forward(k).start()
 
     def send_flags():
@@ -596,9 +649,8 @@
             send_flag(slot).start()
 
     def relay_home():
-        for k in range(1, half):
-            give_relay(k).wait_recv()
-            forward(k).wait_send()
+        all_relay.wait_recv()
+        all_forward.wait_send()
         closed = jnp.dot(
             inbox[:, width : width + far_rows],
             collected[...],
@@ -634,9 +686,8 @@
         return done
 
     def direct_chunk(chosen_slots):
-        for slot in chosen_slots:
-            if slot > 0:
-                dispatch(slot).wait_recv()
+        for group in sorted({slot // plane for slot in chosen_slots}):
+            landed(group).wait_recv()
         start = rows_of(chosen_slots[0])[0]
         done = expert(start, sum(rows_of(slot)[1] for slot in chosen_slots))
         for slot in chosen_slots:
@@ -646,27 +697,22 @@
                 returned[block(0), :] = done[:cap]
 
     def share_flags():
-        for slot in range(1, n):
-            send_flag(slot).wait_recv()
+        all_flags.wait_recv()
         group_out[...] = jnp.max(flags_in[...], axis=0)
-        for slot in range(1, n):
-            send_flag(slot).wait_send()
+        all_flags.wait_send()
         swap_flag.start()
 
     def drain():
         send_pouch.wait_send()
-        for slot in range(1, n):
-            dispatch(slot).wait_send()
-        for pair in shares:
-            for share in pair:
-                share.wait_send()
+        all_sent().wait_send()
+        sent_in.wait_send()
+        sent_out.wait_send()
 
     def relayed_chunk():
-        for k in range(1, half):
-            forward(k).wait_recv()
+        all_forward.wait_recv()
         done = expert(direct_rows, far_rows)
         collected[extra(0), :] = done[:base]
-        for k in range(1, half):
+        for k in reversed(range(1, half)):
             give_relay(k).start()
 
     groups = {
@@ -674,6 +720,7 @@
         "n1": range(plane, half),
         "fa": range(half, half + plane),
         "fb": range(half + plane, n),
+        "ff": range(half, n),
     }
     steps = {
         "pouch": send_pouch.start,
@@ -709,12 +756,9 @@
             here = pl.ds(direct_rows, spare)
             back_pouch.wait_recv()
         else:
-            for slot in groups[name]:
-                if slot > 0:
-                    give_back(slot).wait_recv()
-            here = pl.ds(
-                rows_of(groups[name][0])[0], sum(rows_of(slot)[1] for slot in groups[name])
-            )
+            for group in sorted({slot // plane for slot in groups[name]}):
+                came_back(group).wait_recv()
+            here = rows_in_all(groups[name][0], groups[name][-1] + 1)
         arrived += jnp.dot(
             place[:, here], returned[here, :], preferred_element_type=jnp.float32
         )
@@ -722,10 +766,8 @@
     out_ref[...] = sums.astype(jnp.bfloat16)
 
     back_pouch.wait_send()
-    for k in range(1, half):
-        give_relay(k).wait_send()
-    for slot in range(1, n):
-        give_back(slot).wait_send()
+    all_relay.wait_send()
+    all_given().wait_send()
     tell.wait()
 
 
@@ -772,20 +814,20 @@
             pltpu.VMEM((8, 128), jnp.float32),
             pltpu.SMEM((1, 1), jnp.int32),
             sems((6,)),
+            sems((2,)),
             sems((2, hidden // TILE)),
-            sems((2, hidden // TILE)),
-            sems((n,)),
-            sems((n,)),
-            sems((n,)),
-            sems((n,)),
-            sems((half,)),
-            sems((half,)),
-            sems((half,)),
-            sems((half,)),
+            sems((1,)),
+            sems((4,)),
+            sems((1,)),
+            sems((4,)),
+            sems((1,)),
+            sems((1,)),
+            sems((1,)),
+            sems((1,)),
             sems((2,)),
             sems((2,)),
-            sems((n,)),
-            sems((n,)),
+            sems((2,)),
+            sems((2,)),
             flags((2,)),
             flags((4,)),
         ],

time: 47.4 us -> 45 us (0.949)
  Pallas kernels: 45.3 us -> 43.3 us
    pallas_call x1, Pallas kernels: 45.3 us -> 43.3 us  [with_relay(): pl.pallas_call(functools.partial(relay_kernel, n, cap, spare), out_shape=...]
where the time goes in v3:
time: 45 us; the launch traced here: 44.9 us
  Pallas kernels  43.3 us (96%)
  local copies, waits for them, and re-layouts  0.81 us (2%)
  between operations  0.74 us (2%)
    pallas_call x1, Pallas kernels, with_relay(): pl.pallas_call(functools.partial(relay_kernel, n, cap, spare), out_shape=...  43.3 us

profile of v3, /device:TPU:0, one launch (start us, length us, event | category | flops | bytes accessed | tf_op | source)
XLA Modules:
  0.0 44.9 jit_solution(3963501436618493281)
XLA Ops:
  0.0 0.0 copy-start
  0.0 0.0 copy-start.1
  0.0 0.0 copy-start.2
  0.0 0.0 copy-start.3
  0.0 43.3 %shard_map.66 = (bf16[256,1024]{1,0:T(8,128)(2,1)S(1)}, s32[1,1]{1,0:T(1,128)}) custom-call(s32[1,256]{1,0:T(1,128)} %bitcast.5, s32[1,256]{1,0:T(1,128)} %bitcast.7, bf16[256,1024]{1,0:T(8,128)(2,1)} %tokens_hbm.1, bf16[16,1024]{1,0:T(8,128)(2,1)} %centroids_hbm.1, bf16[1,1024,2048]{2,1,0:T(8,128)(2,1)} %w_in_ref.1, bf16[1,2048,1024]{2,1,0:T(8,128)(2,1)} %w_out_ref.1), custom_call_target="tpu_custom_call" | custom-call | tf_op jit(solution)/shard_map/pallas_call | solution.py:786
  44.0 0.0 copy-done
  44.0 0.0 copy-done.1
  44.1 0.0 copy-done.2
  44.1 0.0 copy-done.3
  44.1 0.8 %copy.12 = bf16[256,1024]{1,0:T(8,128)(2,1)} copy(bf16[256,1024]{1,0:T(8,128)(2,1)S(1)} %get-tuple-element.31) | data formatting | bytes 1048576
  (1 shorter events, 0.0 us)
Async XLA Ops:
  0.0 44.0 %copy-start = (bf16[256,1024]{1,0:T(8,128)(2,1)S(1)}, bf16[256,1024]{1,0:T(8,128)(2,1)}, u32[]{:S(2)}) copy-start(bf16[256,1024]{1,0:T(8,128)(2,1)} %tokens_hbm.1) | copy-start | bytes 1572868
  0.0 44.0 %copy-start.1 = (bf16[16,1024]{1,0:T(8,128)(2,1)S(1)}, bf16[16,1024]{1,0:T(8,128)(2,1)}, u32[]{:S(2)}) copy-start(bf16[16,1024]{1,0:T(8,128)(2,1)} %centroids_hbm.1) | copy-start | bytes 98308
  0.0 44.1 %copy-start.2 = (s32[256]{0:T(256)S(1)}, s32[256]{0:T(256)}, u32[]{:S(2)}) copy-start(s32[256]{0:T(256)} %param.9) | copy-start | bytes 3076
  0.0 44.1 %copy-start.3 = (s32[256]{0:T(256)S(1)}, s32[256]{0:T(256)}, u32[]{:S(2)}) copy-start(s32[256]{0:T(256)} %param.10) | copy-start | bytes 3076

commit v4 on v3

--- a/solution.py
+++ b/solution.py
@@ -5,6 +5,7 @@
 from jax import lax
 from jax.experimental import pallas as pl
 from jax.experimental.pallas import tpu as pltpu
+from jax.extend.core.primitives import cond_p
 from jax.sharding import PartitionSpec as P
 
 MESH = pl.DeviceIdType.MESH
@@ -842,13 +843,12 @@
         w_in,
         w_out,
     )
-    return lax.switch(
-        spill[0, 0],
-        [
-            lambda: out,
-            lambda: in_one_kernel(n, tokens, expert_ids, slot_ids, centroids, w_in, w_out),
-        ],
-    )
+    operands = (out, tokens, expert_ids, slot_ids, centroids, w_in, w_out)
+    branches = (
+        jax.make_jaxpr(lambda ready, *rest: ready)(*operands),
+        jax.make_jaxpr(lambda ready, *rest: in_one_kernel(n, *rest))(*operands),
+    )
+    return cond_p.bind(spill[0, 0], *operands, branches=branches)[0]
 
 
 def in_plain_ops(tokens, expert_ids, slot_ids, centroids, w_in, w_out):

time: 45 us -> 45 us (level)
  loops' own time: 0.01 us -> 0.7 us
  between operations: 0.74 us -> 0.05 us
    another operation x1, loops' own time: 0.01 us -> 0.7 us  [with_relay(): return cond_p.bind(spill[0, 0], *operands, branches=branches)[0]]
where the time goes in v4:
time: 45 us; the launch traced here: 44.9 us
  Pallas kernels  43.3 us (96%)
  local copies, waits for them, and re-layouts  0.81 us (2%)
  loops' own time  0.7 us (2%)
    pallas_call x1, Pallas kernels, with_relay(): pl.pallas_call(functools.partial(relay_kernel, n, cap, spare), out_shape=...  43.3 us

profile of v4, /device:TPU:0, one launch (start us, length us, event | category | flops | bytes accessed | tf_op | source)
XLA Modules:
  0.0 44.9 jit_solution(12361193728176061625)
XLA Ops:
  0.0 0.0 copy-start
  0.0 0.0 copy-start.1
  0.0 0.0 copy-start.2
  0.0 0.0 copy-start.3
  0.0 43.3 %shard_map.66 = (bf16[256,1024]{1,0:T(8,128)(2,1)S(1)}, s32[1,1]{1,0:T(1,128)}) custom-call(s32[1,256]{1,0:T(1,128)} %bitcast.5, s32[1,256]{1,0:T(1,128)} %bitcast.7, bf16[256,1024]{1,0:T(8,128)(2,1)} %tokens_hbm.1, bf16[16,1024]{1,0:T(8,128)(2,1)} %centroids_hbm.1, bf16[1,1024,2048]{2,1,0:T(8,128)(2,1)} %w_in_ref.1, bf16[1,2048,1024]{2,1,0:T(8,128)(2,1)} %w_out_ref.1), custom_call_target="tpu_custom_call" | custom-call | tf_op jit(solution)/shard_map/pallas_call | solution.py:787
  43.3 0.0 copy-done
  43.4 0.0 copy-done.1
  43.4 0.0 copy-done.2
  43.4 0.0 copy-done.3
  43.4 0.7 %conditional.1 = (bf16[256,1024]{1,0:T(8,128)(2,1)S(1)}) conditional(s32[]{:T(128)} %bitcast.4, bf16[256,1024]{1,0:T(8,128)(2,1)S(1)} %get-tuple-element.30, (s32[256]{0:T(256)S(1)}, s32[256]{0:T(256)S(1)}, bf16[256,1024]{1,0:T(8,128)(2,1)S(1)}, bf16[16,1024]{1,0:T(8,128)(2,1)S(1)}, bf16[1,1024,2048]{2,1,0:T(8,128)(2,1)}, ...), branch_computations={%region_0.0_spmd, %region_1.0_spmd} | conditional | bytes 8 | solution.py:851
  44.1 0.8 %copy.12 = bf16[256,1024]{1,0:T(8,128)(2,1)} copy(bf16[256,1024]{1,0:T(8,128)(2,1)S(1)} %get-tuple-element.31) | data formatting | bytes 1048576
Async XLA Ops:
  0.0 43.4 %copy-start = (bf16[256,1024]{1,0:T(8,128)(2,1)S(1)}, bf16[256,1024]{1,0:T(8,128)(2,1)}, u32[]{:S(2)}) copy-start(bf16[256,1024]{1,0:T(8,128)(2,1)} %tokens_hbm.1) | copy-start | bytes 1572868
  0.0 43.4 %copy-start.1 = (bf16[16,1024]{1,0:T(8,128)(2,1)S(1)}, bf16[16,1024]{1,0:T(8,128)(2,1)}, u32[]{:S(2)}) copy-start(bf16[16,1024]{1,0:T(8,128)(2,1)} %centroids_hbm.1) | copy-start | bytes 98308
  0.0 43.4 %copy-start.2 = (s32[256]{0:T(256)S(1)}, s32[256]{0:T(256)}, u32[]{:S(2)}) copy-start(s32[256]{0:T(256)} %param.9) | copy-start | bytes 3076
  0.0 43.4 %copy-start.3 = (s32[256]{0:T(256)S(1)}, s32[256]{0:T(256)}, u32[]{:S(2)}) copy-start(s32[256]{0:T(256)} %param.10) | copy-start | bytes 3076
